TPU v7x, 128 devices: a whole 4x4x4 slice. The times are simulated.
128 devices in a mesh: seq: 16 (over x, y_lo, core), tp: 8 (over z, y_hi).
Axes of the slice: x: 4, y: 4 (y_hi: 2, y_lo: 2; y = y_hi * 2 + y_lo), z: 4, core: 2. Of those that a mesh axis runs over, the one named last changes fastest.
Arguments:
- x_old: bfloat16 [8192, 4608], P('seq', 'tp'), may hold values from -6 to 6
- old_blocks: int32 [16], replicated, may hold values from 1 to 4, 32 in all
- new_blocks: int32 [16], replicated, may hold values from 1 to 4, 32 in all
- order: int32 [16], replicated, may hold values from 0 to 15, as said below
- pre_gain: float32 [4608], replicated, may hold values from 0.25 to 1.75
- post_gain: float32 [4608], replicated, may hold values from 0.25 to 1.75
- w_query: bfloat16 [4608, 4096], P('seq', 'tp'), may hold values from -0.59765625 to 0.59765625
- w_key: bfloat16 [4608, 2048], P('seq', 'tp'), may hold values from -0.09375 to 0.09375
- w_value: bfloat16 [4608, 2048], P('seq', 'tp'), may hold values from -0.09375 to 0.09375
- w_out_t: bfloat16 [4608, 4096], P('seq', 'tp'), may hold values from -0.09375 to 0.09375
Outputs:
- layer_out: bfloat16 [8192, 4608], P(('seq', 'tp'))
Inputs may be any that keep to these rules, and one draw needn't show every extreme that they name: `old_blocks`: counts of 128-row blocks, at least one each; they sum to 32, and the largest is exactly 4. `new_blocks`: counts of 128-row blocks, at least one each; they sum to 32, and the largest is exactly 4. A permutation of the seq indices with order[15] = 0 and order[7] = 15; the other indices, taken in increasing order, hold 1 to 14 in increasing order, except that aligned pairs of them (first and second, third and fourth, and so on) are swapped or not, pair by pair.
All inputs are finite; a program needn't handle non-finite values.
Results may differ from a plain program's by a relative error of at most 0.013.
Values may be sent and summed in bfloat16 or wider, within the bound.
A program may use at most 128 MiB of HBM per device.

v0:
```python
import math
import jax
import jax.numpy as jnp
from jax import lax
from jax.sharding import Mesh
from jax.sharding import PartitionSpec as P

D = 4608
HEADS = 32
HEAD = 128
BLOCK = 128
TP = ("tp_0", "tp_1")
SEQ_TP = ("seq", "tp_0", "tp_1")
EPS = 1e-06


def in_one_piece(arrays, axis, dim, along):
    widths = [a.shape[along] for a in arrays]
    both = jnp.concatenate(arrays, axis=along)
    whole = lax.all_gather(both, axis, axis=dim, tiled=True)
    return tuple(jnp.split(whole, [sum(widths[:k]) for k in range(1, len(widths))], axis=along))


def sum_by_axis(terms, axes):
    so_far = terms.astype(jnp.bfloat16)
    for axis in axes:
        so_far = lax.psum_scatter(so_far, axis, scatter_dimension=0, tiled=True)
    return so_far.astype(jnp.float32)


def offsets(blocks):
    return (jnp.cumsum(blocks) - blocks) * BLOCK


def rotate(values, places):
    half = values.shape[-1] // 2
    inverse = jnp.exp(
        jnp.arange(half, dtype=jnp.float32) * (-2.0 * math.log(10000.0) / values.shape[-1])
    )
    angles = places.astype(jnp.float32)[:, None] * inverse[None, :]
    cosine = jnp.cos(angles)[:, None, :]
    sine = jnp.sin(angles)[:, None, :]
    first = values[..., :half]
    second = values[..., half:]
    return jnp.concatenate(
        [first * cosine - second * sine, second * cosine + first * sine], axis=-1
    )


def rms_scale(values, gain):
    return values * lax.rsqrt(jnp.mean(values * values, axis=-1, keepdims=True) + EPS) * gain


def per_device(
    x_old, old_blocks, new_blocks, order, pre_gain, post_gain, w_query, w_key, w_value, w_out_t
):
    seq_count = lax.axis_size("seq")
    tp_count = lax.axis_size(TP)
    capacity = x_old.shape[0]
    seq_index = lax.axis_index("seq")
    tp_index = lax.axis_index(TP)
    old_start = offsets(old_blocks)
    new_start = offsets(new_blocks)
    new_count = new_blocks * BLOCK
    slot_ids = jnp.arange(capacity, dtype=jnp.int32)
    device_ids = jnp.arange(seq_count, dtype=jnp.int32)
    my_start = new_start[seq_index]
    my_count = new_count[seq_index]
    gathered = lax.all_gather(x_old, "seq", axis=0, tiled=True)
    wanted = my_start + slot_ids
    shard = jnp.sum((old_start[None, :] <= wanted[:, None]).astype(jnp.int32), axis=1) - 1
    match_shard = device_ids[None, :] == shard[:, None]
    holder = jnp.sum(
        device_ids[None, :] * (order[None, :] == shard[:, None]).astype(jnp.int32), axis=1
    )
    shard_start = jnp.sum(jnp.where(match_shard, old_start[None, :], 0), axis=1)
    source = jnp.clip(holder * capacity + wanted - shard_start, 0, seq_count * capacity - 1)
    own_rows = jnp.where(
        (slot_ids < my_count)[:, None], gathered[source], jnp.zeros((), jnp.bfloat16)
    )
    full_rows = lax.all_gather(own_rows, TP, axis=1, tiled=True)
    resident_f = full_rows.astype(jnp.float32)
    normed = rms_scale(resident_f, pre_gain).astype(jnp.bfloat16)
    query_full, key_full, value_full, out_full = in_one_piece(
        (w_query, w_key, w_value, w_out_t), "seq", 0, 1
    )
    query_raw = jnp.dot(normed, query_full, preferred_element_type=jnp.float32)
    key_raw = jnp.dot(normed, key_full, preferred_element_type=jnp.float32)
    value_raw = jnp.dot(normed, value_full, preferred_element_type=jnp.float32)
    local_heads = query_raw.shape[1] // HEAD
    local_kv = key_raw.shape[1] // HEAD
    group = local_heads // local_kv
    positions = my_start + slot_ids
    query_rot = (
        rotate(query_raw.reshape(capacity, local_heads, HEAD), positions) * (D // HEADS) ** (-0.5)
    ).astype(jnp.bfloat16)
    query_four = query_rot.reshape(capacity, local_kv, group, HEAD)
    key_rot = (
        rotate(key_raw.reshape(capacity, local_kv, HEAD), positions)
        .astype(jnp.bfloat16)
        .reshape(capacity, local_kv * HEAD)
    )
    value_b = value_raw.astype(jnp.bfloat16)
    start_state = (
        jnp.zeros((capacity, local_kv, group, HEAD), jnp.float32),
        jnp.zeros((local_kv, group, capacity), jnp.float32),
    )
    key_piece, value_piece = in_one_piece((key_rot, value_b), "seq", 0, 1)
    piece_rows = key_piece.shape[0]

    def one_block(carry_in, offset):
        numer, denom = carry_in
        key_block = lax.dynamic_slice_in_dim(key_piece, offset, capacity, 0).reshape(
            capacity, local_kv, HEAD
        )
        value_block = lax.dynamic_slice_in_dim(value_piece, offset, capacity, 0).reshape(
            capacity, local_kv, HEAD
        )
        global_ids = offset + jnp.arange(capacity, dtype=jnp.int32)
        owner = global_ids // capacity
        within = global_ids - owner * capacity
        onehot = owner[:, None] == device_ids[None, :]
        key_pos = jnp.sum(jnp.where(onehot, new_start[None, :], 0), axis=1) + within
        key_live = within < jnp.sum(jnp.where(onehot, new_count[None, :], 0), axis=1)
        allowed = key_live[None, :] & (key_pos[None, :] <= positions[:, None])
        score = jnp.einsum(
            "qcgd,kcd->cgqk", query_four, key_block, preferred_element_type=jnp.float32
        )
        weight = jnp.where(allowed[None, None, :, :], jnp.exp(50.0 * jnp.tanh(score / 50.0)), 0.0)
        denom = denom + jnp.sum(weight, axis=3)
        numer = numer + jnp.einsum(
            "cgqk,kcd->qcgd",
            weight.astype(jnp.bfloat16),
            value_block,
            preferred_element_type=jnp.float32,
        )
        return (numer, denom)

    numer, denom = lax.fori_loop(
        0,
        piece_rows // capacity,
        lambda turn, state: one_block(state, turn * capacity),
        start_state,
    )
    context = (
        (numer / jnp.transpose(denom, (2, 0, 1))[:, :, :, None])
        .astype(jnp.bfloat16)
        .reshape(capacity, local_heads * HEAD)
    )
    share = capacity // tp_count
    projected = sum_by_axis(
        lax.dot_general(
            context, out_full, (((1,), (1,)), ((), ())), preferred_element_type=jnp.float32
        ),
        TP,
    )
    first_row = tp_index * share
    residual = lax.dynamic_slice_in_dim(resident_f, first_row, share, 0)
    refreshed = residual + rms_scale(projected, post_gain)
    live = first_row + jnp.arange(share, dtype=jnp.int32) < my_count
    return jnp.where(live[:, None], refreshed, 0.0).astype(jnp.bfloat16)


def solution(mesh):
    torus = Mesh(mesh.devices.reshape(mesh.shape["seq"], 4, 2), ("seq", "tp_0", "tp_1"))
    in_specs = (
        P("seq", TP),
        P(),
        P(),
        P(),
        P(),
        P(),
        P("seq", TP),
        P("seq", TP),
        P("seq", TP),
        P("seq", TP),
    )
    out_specs = P(SEQ_TP, None)
    return jax.shard_map(
        per_device, mesh=torus, in_specs=in_specs, out_specs=out_specs, check_vma=False
    )
```

profile of v0, /device:TPU:1, one launch (start us, length us, event | category | flops | bytes accessed | tf_op | source)
XLA Modules:
  0.0 493.3 jit_solution(17339269859793845897)
XLA Ops:
  6.5 2.2 copy.36
  15.9 58.7 %all-gather.5.cloned.1.call-done = bf16[8192,576]{1,0:T(8,128)(2,1)} async-done(((bf16[512,576]{1,0:T(8,128)(2,1)}), bf16[8192,576]{1,0:T(8,128)(2,1)}) %all-gather.5.cloned.1.call-update) | async-done | bytes 9437200 | tf_op jit(solution)/shard_map/all_gather | solution.py:69
  74.6 7.5 %gather_fusion = bf16[512,576]{1,0:T(8,128)(2,1)S(1)} fusion(bf16[8192,576]{1,0:T(8,128)(2,1)} %all-gather.5.cloned.1.call-done, s32[1024]{0:T(1024)S(1)} %pad_clamp_fusion), kind=kCustom, calls=%fused_computation | custom fusion | bytes 1181696 | tf_op jit(solution)/shard_map/gather | solution.py:79
  85.0 73.8 %all-gather.7.cloned.1.call-done = bf16[512,4608]{0,1:T(8,128)(2,1)} async-done(((bf16[512,576]{0,1:T(8,128)(2,1)}), bf16[512,4608]{0,1:T(8,128)(2,1)}) %all-gather.7.cloned.1.call-update) | async-done | bytes 4718608 | tf_op jit(solution)/shard_map/all_gather | solution.py:81
  158.8 6.8 %copy.40 = bf16[512,4608]{1,0:T(8,128)(2,1)} copy(bf16[512,4608]{0,1:T(8,128)(2,1)} %all-gather.7.cloned.1.call-done) | data formatting | bytes 9437184 | tf_op jit(solution)/shard_map/all_gather | solution.py:81
  165.6 3.3 multiply_reduce_fusion
  168.9 69.7 %all-gather.9.cloned.1.call-done = bf16[4608,1536]{1,0:T(8,128)(2,1)} async-done(((bf16[288,1536]{1,0:T(8,128)(2,1)}), bf16[4608,1536]{1,0:T(8,128)(2,1)}) %all-gather.9.cloned.1.call-update) | async-done | bytes 14155792 | tf_op jit(solution)/shard_map/all_gather | solution.py:20
  238.6 4.8 fusion.32
  243.6 4.8 fusion.34
  249.5 6.5 %fusion.28 = f32[512,512]{0,1:T(8,128)S(1)} fusion(bf16[4608,1536]{1,0:T(8,128)(2,1)} %all-gather.9.cloned.1.call-done, f32[4608]{0:T(1024)S(1)} %copy-done.6, f32[512]{0:T(512)S(1)} %add_rsqrt_fusion, bf16[512,4608]{1,0:T(8,128)(2,1)} %copy.40), kind=kOutput, calls=%fused_computation.39 | convolution fusion | flops 2425356288 | bytes 10506240 | tf_op jit(solution)/shard_map/dot_general | solution.py:87
  257.3 45.0 %all-gather.11.cloned.1.call-done = bf16[8192,512]{0,1:T(8,128)(2,1)} async-done(((bf16[512,512]{0,1:T(8,128)(2,1)}), bf16[8192,512]{0,1:T(8,128)(2,1)}) %all-gather.11.cloned.1.call-update) | async-done | bytes 8388624 | tf_op jit(solution)/shard_map/all_gather | solution.py:20
  302.2 5.9 %fusion.44 = (bf16[8192,256]{0,1:T(8,128)(2,1)}, bf16[8192,256]{0,1:T(8,128)(2,1)}) fusion(bf16[8192,512]{0,1:T(8,128)(2,1)} %all-gather.11.cloned.1.call-done), kind=kLoop, calls=%fused_computation.84 | loop fusion | bytes 16777216 | tf_op jit(solution)/shard_map/split | solution.py:21
  308.2 88.0 %while.18 = (s32[]{:T(128)}, f32[512,2,2,128]{0,3,2,1:T(8,128)S(1)}, f32[2,2,512]{2,1,0:T(2,128)S(1)}, bf16[8192,256]{0,1:T(8,128)(2,1)}, s32[16]{0:T(128)S(1)},...) while((s32[]{:T(128)}, ...), condition=%wide.region_10.11_spmd.clone, body=%wide.region_6.10_spmd.clone.sunk | while | flops 546378240 | bytes 13423954 | solution.py:139
  310.2 1.8 fusion.63
  312.0 1.6 fusion.64
  315.7 1.8 fusion.63
  317.5 1.6 fusion.64
  321.2 1.8 fusion.63
  323.0 1.6 fusion.64
  326.7 1.8 fusion.63
  328.5 1.6 fusion.64
  332.2 1.8 fusion.63
  334.0 1.6 fusion.64
  337.7 1.8 fusion.63
  339.5 1.6 fusion.64
  343.2 1.8 fusion.63
  345.0 1.6 fusion.64
  348.7 1.8 fusion.63
  350.5 1.6 fusion.64
  354.2 1.8 fusion.63
  356.0 1.6 fusion.64
  359.7 1.8 fusion.63
  361.5 1.6 fusion.64
  365.2 1.8 fusion.63
  367.0 1.6 fusion.64
  370.7 1.8 fusion.63
  376.2 1.8 fusion.63
  378.0 1.6 fusion.64
  381.7 1.8 fusion.63
  383.5 1.6 fusion.64
  387.2 1.8 fusion.63
  389.0 1.6 fusion.64
  392.7 1.8 fusion.63
  396.3 6.7 %convolution_convert_fusion = bf16[512,4608]{1,0:T(8,128)(2,1)} fusion(bf16[512,512]{0,1:T(8,128)(2,1)S(1)} %bitcast.65, bf16[4608,1536]{1,0:T(8,128)(2,1)} %all-gather.9.cloned.1.call-done), kind=kOutput, calls=%fused_computation.37 | convolution fusion | flops 2418278400 | bytes 9961472 | tf_op jit(solution)/shard_map/dot_general | solution.py:152
  403.1 51.9 %reduce-scatter.3.cloned.1.call-done = bf16[128,4608]{1,0:T(8,128)(2,1)} async-done(((bf16[512,4608]{1,0:T(8,128)(2,1)}), bf16[128,4608]{1,0:T(8,128)(2,1)}) %reduce-scatter.3.cloned.1.call-update) | async-done | bytes 1179664 | tf_op jit(solution)/shard_map/reduce_scatter | solution.py:27
  455.6 7.2 %convert_element_type.53 = f32[512,4608]{1,0:T(8,128)} convert(bf16[512,4608]{1,0:T(8,128)(2,1)} %copy.40) | non-fusion elementwise | flops 2359296 | bytes 14155776 | tf_op jit(solution)/shard_map/convert_element_type | solution.py:82
  462.8 19.7 %reduce-scatter.5.cloned.1.call-done = bf16[64,4608]{1,0:T(8,128)(2,1)} async-done(((bf16[128,4608]{1,0:T(8,128)(2,1)}), bf16[64,4608]{1,0:T(8,128)(2,1)}) %reduce-scatter.5.cloned.1.call-update) | async-done | bytes 589840 | tf_op jit(solution)/shard_map/reduce_scatter | solution.py:27
  483.9 2.6 fusion.41
  (177 shorter events, 50.3 us)
Async XLA Ops:
  6.5 68.0 %all-gather.5.cloned.1.call-start = ((), (), s32[]{:S(2)}) async-start(), calls=%async_computation.2 | async-start | bytes 11141120 | tf_op jit(solution)/shard_map/all_gather | solution.py:69
  8.7 74.6 %copy-start.1 = (bf16[288,512]{1,0:T(8,128)(2,1)S(1)}, bf16[288,512]{1,0:T(8,128)(2,1)}, u32[]{:S(2)}) copy-start(bf16[288,512]{1,0:T(8,128)(2,1)} %param.21) | copy-start | bytes 884740
  8.7 74.6 %copy-start.2 = (bf16[288,512]{1,0:T(8,128)(2,1)S(1)}, bf16[288,512]{1,0:T(8,128)(2,1)}, u32[]{:S(2)}) copy-start(bf16[288,512]{1,0:T(8,128)(2,1)} %param.18) | copy-start | bytes 884740
  8.8 74.6 %copy-start.3 = (bf16[288,256]{1,0:T(8,128)(2,1)S(1)}, bf16[288,256]{1,0:T(8,128)(2,1)}, u32[]{:S(2)}) copy-start(bf16[288,256]{1,0:T(8,128)(2,1)} %param.20) | copy-start | bytes 442372
  8.8 74.6 %copy-start.4 = (bf16[288,256]{1,0:T(8,128)(2,1)S(1)}, bf16[288,256]{1,0:T(8,128)(2,1)}, u32[]{:S(2)}) copy-start(bf16[288,256]{1,0:T(8,128)(2,1)} %param.19) | copy-start | bytes 442372
  8.8 150.0 %all-gather.7.cloned.1.call-start = ((), (), s32[]{:S(2)}) async-start(), calls=%async_computation.3 | async-start | bytes 5308416 | tf_op jit(solution)/shard_map/all_gather | solution.py:81
  83.3 155.3 %all-gather.9.cloned.1.call-start = ((), (), s32[]{:S(2)}) async-start(), calls=%async_computation.4 | async-start | bytes 15040512 | tf_op jit(solution)/shard_map/all_gather | solution.py:20
  84.4 217.9 %all-gather.11.cloned.1.call-start = ((), (), s32[]{:S(2)}) async-start(), calls=%async_computation.5 | async-start | bytes 8912896 | tf_op jit(solution)/shard_map/all_gather | solution.py:20
  165.6 73.0 %copy-start.6 = (f32[4608]{0:T(1024)S(1)}, f32[4608]{0:T(1024)}, u32[]{:S(2)}) copy-start(f32[4608]{0:T(1024)} %param.16) | copy-start | bytes 55300
  249.3 205.7 %reduce-scatter.3.cloned.1.call-start = ((), (), s32[]{:S(2)}) async-start(), calls=%async_computation.6 | async-start | bytes 5898240 | tf_op jit(solution)/shard_map/reduce_scatter | solution.py:27
  257.3 50.9 %copy-start = (f32[512,2,2,128]{0,3,2,1:T(8,128)S(1)}, f32[512,2,2,128]{0,3,2,1:T(8,128)}, u32[]{:S(2)}) copy-start(f32[512,2,2,128]{0,3,2,1:T(8,128)} %custom-call) | copy-start | bytes 3145732
  403.0 79.5 %reduce-scatter.5.cloned.1.call-start = ((), (), s32[]{:S(2)}) async-start(), calls=%async_computation.7 | async-start | bytes 1769472 | tf_op jit(solution)/shard_map/reduce_scatter | solution.py:27
  455.6 28.2 %copy-start.5 = (f32[4608]{0:T(1024)S(1)}, f32[4608]{0:T(1024)}, u32[]{:S(2)}) copy-start(f32[4608]{0:T(1024)} %param.17) | copy-start | bytes 55300
Sparse Core Ops, SparseCore 0:
  9.0 65.4 all-gather.4
  83.4 75.3 all-gather.6
  160.5 78.0 all-gather.8
  249.4 52.8 all-gather.10
  403.1 51.7 reduce-scatter.2
  457.1 25.3 reduce-scatter.4
where the time goes:
time: 494 us; the launch traced here: 493 us
  waiting for transfers between devices  319 us (65%)
  matrix products  77.3 us (16%)
  local copies, waits for them, and re-layouts  44 us (9%)
  other arithmetic  37.9 us (8%)
  between operations  13.8 us (3%)
    all_gather x2, waiting for transfers between devices, in_one_piece(): whole = lax.all_gather(both, axis, axis=dim, tiled=True)  115 us
    all_gather x1, waiting for transfers between devices, per_device(): full_rows = lax.all_gather(own_rows, TP, axis=1, tiled=True)  73.8 us
    reduce_scatter x2, waiting for transfers between devices, sum_by_axis(): so_far = lax.psum_scatter(so_far, axis, scatter_dimension=0, tiled=True)  71.6 us
    all_gather x1, waiting for transfers between devices, per_device(): gathered = lax.all_gather(x_old, 'seq', axis=0, tiled=True)  58.7 us
    dot_general x16, matrix products, one_block(): jnp.einsum('qcgd,kcd->cgqk', query_four, key_block, preferred_element_typ...  28.1 us
    dot_general x16, matrix products, one_block(): jnp.einsum('cgqk,kcd->qcgd', weight.astype(jnp.bfloat16), value_block, pr...  26.3 us
    dynamic_slice x16, local copies, waits for them, and re-layouts, one_block(): lax.dynamic_slice_in_dim(key_piece, offset, capacity, 0)  17.2 us
    add x17, other arithmetic, per_device(): wanted = my_start + slot_ids  9.9 us
  transfers between devices with their start and end apart: 6, of which 6 were waited for; matrix products, arithmetic and copies ran while one was open for 7% of the time, Pallas kernels for 0%

commit v1 on v0

--- a/solution.py
+++ b/solution.py
@@ -66,7 +66,9 @@
     device_ids = jnp.arange(seq_count, dtype=jnp.int32)
     my_start = new_start[seq_index]
     my_count = new_count[seq_index]
-    gathered = lax.all_gather(x_old, "seq", axis=0, tiled=True)
+    gathered = jnp.concatenate(
+        lax.all_to_all(jnp.stack([x_old] * lax.axis_size("seq")), "seq", 0, 0), axis=0
+    )
     wanted = my_start + slot_ids
     shard = jnp.sum((old_start[None, :] <= wanted[:, None]).astype(jnp.int32), axis=1) - 1
     match_shard = device_ids[None, :] == shard[:, None]

time: 494 us -> 663 us (1.34)
  waiting for transfers between devices: 319 us -> 407 us
  matrix products: 77.3 us -> 137 us
  local copies, waits for them, and re-layouts: 44 us -> 60.2 us
  starting transfers between devices: 0.39 us -> 7.33 us
    all_to_all x0 -> x1, waiting for transfers between devices: none -> 145 us  [per_device(): lax.all_to_all(jnp.stack([x_old] * lax.axis_size('seq')), 'seq', 0, 0)]
    all_gather x1 -> x0, waiting for transfers between devices: 58.7 us -> none  [per_device(): gathered = lax.all_gather(x_old, 'seq', axis=0, tiled=True)]
    dot_general x16, matrix products: 26.3 us -> 59.2 us  [one_block(): jnp.einsum('cgqk,kcd->qcgd', weight.astype(jnp.bfloat16), value_block, pr...]
    dot_general x16, matrix products: 28.1 us -> 54.5 us  [one_block(): jnp.einsum('qcgd,kcd->cgqk', query_four, key_block, preferred_element_typ...]
    all_to_all x0 -> x1, local copies, waits for them, and re-layouts: none -> 14.1 us  [per_device(): lax.all_to_all(jnp.stack([x_old] * lax.axis_size('seq')), 'seq', 0, 0)]
    all_to_all x0 -> x1, starting transfers between devices: none -> 6.95 us  [per_device(): lax.all_to_all(jnp.stack([x_old] * lax.axis_size('seq')), 'seq', 0, 0)]
  transfers between devices with their start and end apart: 6 -> 6, of which waited for: 6 -> 6; matrix products, arithmetic and copies ran while one was open for 7% -> 5% of each run, Pallas kernels for 0% -> 0%
where the time goes in v1:
time: 663 us; the launch traced here: 662 us
  waiting for transfers between devices  407 us (61%)
  matrix products  137 us (21%)
  local copies, waits for them, and re-layouts  60.2 us (9%)
  other arithmetic  36 us (5%)
  between operations  13.4 us (2%)
  starting transfers between devices  7.33 us (1%)
    all_to_all x1, waiting for transfers between devices, per_device(): lax.all_to_all(jnp.stack([x_old] * lax.axis_size('seq')), 'seq', 0, 0)  145 us
    all_gather x2, waiting for transfers between devices, in_one_piece(): whole = lax.all_gather(both, axis, axis=dim, tiled=True)  115 us
    all_gather x1, waiting for transfers between devices, per_device(): full_rows = lax.all_gather(own_rows, TP, axis=1, tiled=True)  76.3 us
    reduce_scatter x2, waiting for transfers between devices, sum_by_axis(): so_far = lax.psum_scatter(so_far, axis, scatter_dimension=0, tiled=True)  71.6 us
    dot_general x16, matrix products, one_block(): jnp.einsum('cgqk,kcd->qcgd', weight.astype(jnp.bfloat16), value_block, pr...  59.2 us
    dot_general x16, matrix products, one_block(): jnp.einsum('qcgd,kcd->cgqk', query_four, key_block, preferred_element_typ...  54.5 us
    dynamic_slice x16, local copies, waits for them, and re-layouts, one_block(): lax.dynamic_slice_in_dim(key_piece, offset, capacity, 0)  17.1 us
    all_to_all x1, local copies, waits for them, and re-layouts, per_device(): lax.all_to_all(jnp.stack([x_old] * lax.axis_size('seq')), 'seq', 0, 0)  14.1 us
  transfers between devices with their start and end apart: 6, of which 6 were waited for; matrix products, arithmetic and copies ran while one was open for 5% of the time, Pallas kernels for 0%

profile of v1, /device:TPU:1, one launch (start us, length us, event | category | flops | bytes accessed | tf_op | source)
XLA Modules:
  0.0 661.5 jit_solution(13024424873327461294)
XLA Ops:
  6.5 5.6 stack.2
  12.1 6.9 %all-to-all-start = ((bf16[16,512,576]{1,2,0:T(8,128)(2,1)}), bf16[16,512,576]{1,2,0:T(8,128)(2,1)}, u32[]{:S(2)}, u32[]{:S(2)}) async-start(bf16[16,512,576]{1,2,0:T(8,128)(2,1)} %stack.2), calls=%async_computation | async-start | bytes 18874368 | tf_op jit(solution)/shard_map/all_to_all | solution.py:70
  22.9 144.5 %all-to-all-done = bf16[16,512,576]{1,2,0:T(8,128)(2,1)} async-done(((bf16[16,512,576]{1,2,0:T(8,128)(2,1)}), bf16[16,512,576]{1,2,0:T(8,128)(2,1)}, u32[]{:S(2)}, u32[]{:S(2)}) %all-to-all-start) | async-done | bytes 9437216 | tf_op jit(solution)/shard_map/all_to_all | solution.py:70
  167.4 14.1 %copy.36 = bf16[16,512,576]{2,1,0:T(8,128)(2,1)} copy(bf16[16,512,576]{1,2,0:T(8,128)(2,1)} %all-to-all-done) | data formatting | bytes 18874368 | tf_op jit(solution)/shard_map/all_to_all | solution.py:70
  181.5 7.5 %gather_fusion = bf16[512,576]{1,0:T(8,128)(2,1)S(1)} fusion(bf16[8192,576]{1,0:T(8,128)(2,1)} %bitcast.60, s32[1024]{0:T(1024)S(1)} %pad_clamp_fusion), kind=kCustom, calls=%fused_computation | custom fusion | bytes 1181696 | tf_op jit(solution)/shard_map/gather | solution.py:81
  192.0 76.3 %all-gather.4.cloned.1.call-done = bf16[512,4608]{0,1:T(8,128)(2,1)} async-done(((bf16[512,576]{0,1:T(8,128)(2,1)}), bf16[512,4608]{0,1:T(8,128)(2,1)}) %all-gather.4.cloned.1.call-update) | async-done | bytes 4718608 | tf_op jit(solution)/shard_map/all_gather | solution.py:83
  268.3 6.8 %copy.40 = bf16[512,4608]{1,0:T(8,128)(2,1)} copy(bf16[512,4608]{0,1:T(8,128)(2,1)} %all-gather.4.cloned.1.call-done) | data formatting | bytes 9437184 | tf_op jit(solution)/shard_map/all_gather | solution.py:83
  278.4 69.7 %all-gather.6.cloned.1.call-done = bf16[4608,1536]{1,0:T(8,128)(2,1)} async-done(((bf16[288,1536]{1,0:T(8,128)(2,1)}), bf16[4608,1536]{1,0:T(8,128)(2,1)}) %all-gather.6.cloned.1.call-update) | async-done | bytes 14155792 | tf_op jit(solution)/shard_map/all_gather | solution.py:20
  348.1 4.8 fusion.32
  353.0 4.8 fusion.34
  359.0 6.5 fusion.28
  366.7 45.0 %all-gather.8.cloned.1.call-done = bf16[8192,512]{0,1:T(8,128)(2,1)} async-done(((bf16[512,512]{0,1:T(8,128)(2,1)}), bf16[8192,512]{0,1:T(8,128)(2,1)}) %all-gather.8.cloned.1.call-update) | async-done | bytes 8388624 | tf_op jit(solution)/shard_map/all_gather | solution.py:20
  411.7 5.9 fusion.44
  417.7 147.1 %while.18 = (s32[]{:T(128)}, f32[512,2,2,128]{0,3,2,1:T(8,128)S(1)}, f32[2,2,512]{2,1,0:T(2,128)S(1)}, bf16[8192,256]{0,1:T(8,128)(2,1)}, s32[16]{0:T(128)S(1)},...) while((s32[]{:T(128)}, ...), condition=%wide.region_10.11_spmd.clone, body=%wide.region_6.10_spmd.clone.sunk | while | flops 546378240 | bytes 13423946 | solution.py:141
  423.1 3.7 fusion.64
  432.3 3.7 fusion.64
  438.1 3.4 fusion.63
  441.5 3.7 fusion.64
  447.3 3.4 fusion.63
  450.7 3.7 fusion.64
  456.5 3.4 fusion.63
  459.9 3.7 fusion.64
  465.7 3.4 fusion.63
  469.1 3.7 fusion.64
  474.9 3.4 fusion.63
  478.3 3.7 fusion.64
  484.1 3.4 fusion.63
  487.5 3.7 fusion.64
  493.3 3.4 fusion.63
  496.7 3.7 fusion.64
  502.4 3.4 fusion.63
  505.9 3.7 fusion.64
  511.6 3.4 fusion.63
  515.1 3.7 fusion.64
  520.8 3.4 fusion.63
  524.2 3.7 fusion.64
  530.0 3.4 fusion.63
  533.4 3.7 fusion.64
  539.2 3.4 fusion.63
  542.6 3.7 fusion.64
  548.4 3.4 fusion.63
  551.8 3.7 fusion.64
  557.6 3.4 fusion.63
  561.0 3.7 fusion.64
  564.9 6.7 %convolution_convert_fusion = bf16[512,4608]{1,0:T(8,128)(2,1)} fusion(bf16[512,512]{0,1:T(8,128)(2,1)S(1)} %bitcast.67, bf16[4608,1536]{1,0:T(8,128)(2,1)} %all-gather.6.cloned.1.call-done), kind=kOutput, calls=%fused_computation.37 | convolution fusion | flops 2418278400 | bytes 9961472 | tf_op jit(solution)/shard_map/dot_general | solution.py:154
  571.7 51.9 %reduce-scatter.3.cloned.1.call-done = bf16[128,4608]{1,0:T(8,128)(2,1)} async-done(((bf16[512,4608]{1,0:T(8,128)(2,1)}), bf16[128,4608]{1,0:T(8,128)(2,1)}) %reduce-scatter.3.cloned.1.call-update) | async-done | bytes 1179664 | tf_op jit(solution)/shard_map/reduce_scatter | solution.py:27
  624.2 7.2 %convert_element_type.53 = f32[512,4608]{1,0:T(8,128)} convert(bf16[512,4608]{1,0:T(8,128)(2,1)} %copy.40) | non-fusion elementwise | flops 2359296 | bytes 14155776 | tf_op jit(solution)/shard_map/convert_element_type | solution.py:84
  631.4 19.7 %reduce-scatter.5.cloned.1.call-done = bf16[64,4608]{1,0:T(8,128)(2,1)} async-done(((bf16[128,4608]{1,0:T(8,128)(2,1)}), bf16[64,4608]{1,0:T(8,128)(2,1)}) %reduce-scatter.5.cloned.1.call-update) | async-done | bytes 589840 | tf_op jit(solution)/shard_map/reduce_scatter | solution.py:27
  (183 shorter events, 56.3 us)
Async XLA Ops:
  12.1 7.0 %copy-start.6 = (s32[16]{0:T(128)S(1)}, s32[16]{0:T(128)}, u32[]{:S(2)}) copy-start(s32[16]{0:T(128)} %param.14) | copy-start | bytes 196
  12.1 7.3 %copy-start.8 = (s32[16]{0:T(128)S(1)}, s32[16]{0:T(128)}, u32[]{:S(2)}) copy-start(s32[16]{0:T(128)} %param.13) | copy-start | bytes 196
  12.1 10.0 %copy-start.7 = (s32[16]{0:T(128)S(1)}, s32[16]{0:T(128)}, u32[]{:S(2)}) copy-start(s32[16]{0:T(128)} %param.15) | copy-start | bytes 196
  12.1 155.3 %all-to-all-start = ((bf16[16,512,576]{1,2,0:T(8,128)(2,1)}), bf16[16,512,576]{1,2,0:T(8,128)(2,1)}, u32[]{:S(2)}, u32[]{:S(2)}) async-start(bf16[16,512,576]{1,2,0:T(8,128)(2,1)} %stack.2), calls=%async_computation | async-start | bytes 18874368 | tf_op jit(solution)/shard_map/all_to_all | solution.py:70
  19.1 249.2 %all-gather.4.cloned.1.call-start = ((), (), s32[]{:S(2)}) async-start(), calls=%async_computation.3 | async-start | bytes 5308416 | tf_op jit(solution)/shard_map/all_gather | solution.py:83
  181.5 8.9 %copy-start.1 = (bf16[288,512]{1,0:T(8,128)(2,1)S(1)}, bf16[288,512]{1,0:T(8,128)(2,1)}, u32[]{:S(2)}) copy-start(bf16[288,512]{1,0:T(8,128)(2,1)} %param.21) | copy-start | bytes 884740
  181.5 8.9 %copy-start.2 = (bf16[288,512]{1,0:T(8,128)(2,1)S(1)}, bf16[288,512]{1,0:T(8,128)(2,1)}, u32[]{:S(2)}) copy-start(bf16[288,512]{1,0:T(8,128)(2,1)} %param.18) | copy-start | bytes 884740
  181.5 8.9 %copy-start.3 = (bf16[288,256]{1,0:T(8,128)(2,1)S(1)}, bf16[288,256]{1,0:T(8,128)(2,1)}, u32[]{:S(2)}) copy-start(bf16[288,256]{1,0:T(8,128)(2,1)} %param.20) | copy-start | bytes 442372
  181.5 8.9 %copy-start.4 = (bf16[288,256]{1,0:T(8,128)(2,1)S(1)}, bf16[288,256]{1,0:T(8,128)(2,1)}, u32[]{:S(2)}) copy-start(bf16[288,256]{1,0:T(8,128)(2,1)} %param.19) | copy-start | bytes 442372
  190.3 157.7 %all-gather.6.cloned.1.call-start = ((), (), s32[]{:S(2)}) async-start(), calls=%async_computation.4 | async-start | bytes 15040512 | tf_op jit(solution)/shard_map/all_gather | solution.py:20
  191.4 220.3 %all-gather.8.cloned.1.call-start = ((), (), s32[]{:S(2)}) async-start(), calls=%async_computation.5 | async-start | bytes 8912896 | tf_op jit(solution)/shard_map/all_gather | solution.py:20
  275.0 73.0 %copy-start.9 = (f32[4608]{0:T(1024)S(1)}, f32[4608]{0:T(1024)}, u32[]{:S(2)}) copy-start(f32[4608]{0:T(1024)} %param.16) | copy-start | bytes 55300
  358.7 264.8 %reduce-scatter.3.cloned.1.call-start = ((), (), s32[]{:S(2)}) async-start(), calls=%async_computation.6 | async-start | bytes 5898240 | tf_op jit(solution)/shard_map/reduce_scatter | solution.py:27
  366.7 51.0 %copy-start = (f32[512,2,2,128]{0,3,2,1:T(8,128)S(1)}, f32[512,2,2,128]{0,3,2,1:T(8,128)}, u32[]{:S(2)}) copy-start(f32[512,2,2,128]{0,3,2,1:T(8,128)} %custom-call) | copy-start | bytes 3145732
  571.6 79.5 %reduce-scatter.5.cloned.1.call-start = ((), (), s32[]{:S(2)}) async-start(), calls=%async_computation.7 | async-start | bytes 1769472 | tf_op jit(solution)/shard_map/reduce_scatter | solution.py:27
  624.2 28.2 %copy-start.5 = (f32[4608]{0:T(1024)S(1)}, f32[4608]{0:T(1024)}, u32[]{:S(2)}) copy-start(f32[4608]{0:T(1024)} %param.17) | copy-start | bytes 55300
Sparse Core Ops, SparseCore 0:
  190.5 77.7 all-gather.3
  270.0 78.0 all-gather.5
  358.8 52.8 all-gather.7
  571.8 51.7 reduce-scatter.2
  625.8 25.3 reduce-scatter.4
